TPU v7x, 32 devices: a whole 2x2x4 slice. The times are simulated.
32 devices in a mesh: seq: 8 (over z, y), grp: 4 (over x, core).
Axes of the slice: x: 2, y: 2, z: 4, core: 2. Of those that a mesh axis runs over, the one named last changes fastest.
Arguments:
- query_nope: bfloat16 [4, 2, 128, 128], P(None, None, 'seq'), may hold values from -12.859821 to 12.859821
- query_rope: bfloat16 [4, 2, 128, 64], P(None, None, 'seq'), may hold values from -150 to 150
- latent_cache: bfloat16 [4, 8192, 576], P(None, ('seq', 'grp')), may hold values from -5 to 5
- lengths: int32 [4], replicated, may hold values from 4096 to 8192
- key_weight: bfloat16 [128, 128, 512], P('seq'), may hold values from -0.5 to 0.5
- value_weight: bfloat16 [128, 512, 128], P('seq'), may hold values from -0.25 to 0.25
- output_weight: bfloat16 [16384, 7168], P('seq', 'grp'), may hold values from -0.0625 to 0.0625
Outputs:
- mixed: bfloat16 [4, 2, 7168], P(None, None, ('grp', 'seq'))
All inputs are finite; a program needn't handle non-finite values.
Results may differ from a plain program's by a relative error of at most 0.0095.
Values may be sent and summed in bfloat16 or wider, within the bound.
No kernel may reach another device: no remote copies, remote signals or barrier semaphores. Data moves between devices by JAX's collectives and lax.ppermute only.
A program may use at most 64 MiB of HBM per device.

v0:
```python
import jax
import jax.numpy as jnp
from jax import lax
from jax.sharding import PartitionSpec as P

NEGATIVE = -1e30


def joined(part, axis, combine):
    gathered = jax.tree.map(lambda a: lax.all_gather(a, axis), part)

    def take(source):
        return jax.tree.map(lambda a: lax.dynamic_index_in_dim(a, source, 0, False), gathered)

    return lax.fori_loop(
        1, lax.axis_size(axis), lambda source, state: combine(state, take(source)), take(0)
    )


def shard_partial(queries, cache_block, limits, offset, factor, latent_width):
    raw_score = (
        jnp.einsum("bqhd,bpd->bqhp", queries, cache_block, preferred_element_type=jnp.float32)
        * factor
    )
    places = offset + lax.broadcasted_iota(jnp.int32, (1, 1, cache_block.shape[1]), 2)
    visible = places < limits[:, :, None]
    scores = jnp.where(visible[:, :, None, :], raw_score, NEGATIVE)
    maxima = jnp.max(scores, axis=-1)
    powers = jnp.exp(scores - maxima[..., None])
    totals = jnp.sum(powers, axis=-1)
    weights = powers.astype(jnp.bfloat16)
    summed = jnp.einsum(
        "bqhp,bpd->bqhd",
        weights,
        cache_block[:, :, :latent_width],
        preferred_element_type=jnp.float32,
    )
    return (maxima, totals, (summed / totals[..., None]).astype(jnp.bfloat16))


def merge_sources(partials, maxima, totals):
    highest = jnp.max(maxima, axis=0)
    shares = totals * jnp.exp(maxima - highest[None])
    summed = jnp.sum(shares, axis=0)
    numerator = jnp.sum(shares[..., None] * partials.astype(jnp.float32), axis=0)
    return (highest, summed, numerator / summed[..., None])


def merge_tuple(received):
    return merge_sources(received[0], received[1], received[2])


def join_pairs(earlier, later):
    highest = jnp.maximum(earlier[0], later[0])
    left_share = earlier[1] * jnp.exp(earlier[0] - highest)
    right_share = later[1] * jnp.exp(later[0] - highest)
    summed = left_share + right_share
    blended = (left_share[..., None] * earlier[2] + right_share[..., None] * later[2]) / summed[
        ..., None
    ]
    return (highest, summed, blended)


def absorb(query_nope, query_rope, key_weight):
    absorbed = jnp.einsum(
        "bqhn,hnd->bqhd", query_nope, key_weight, preferred_element_type=jnp.float32
    )
    return jnp.concatenate([absorbed.astype(jnp.bfloat16), query_rope], axis=-1)


def up_project(latent_out, value_weight):
    values = jnp.einsum(
        "bqhd,hde->bqhe", latent_out, value_weight, preferred_element_type=jnp.float32
    ).astype(jnp.bfloat16)
    return values.reshape(values.shape[0], values.shape[1], values.shape[2] * values.shape[3])


def shards(query_nope, query_rope, latent_cache, lengths, key_weight, value_weight, output_weight):
    latent_width = key_weight.shape[2]
    factor = float(query_nope.shape[3] + query_rope.shape[3]) ** (-0.5)
    positions = latent_cache.shape[1]
    drafts = query_nope.shape[1]
    offset = (lax.axis_index("seq") * lax.axis_size("grp") + lax.axis_index("grp")) * positions
    limits = lengths[:, None] - drafts + 1 + lax.broadcasted_iota(jnp.int32, (1, drafts), 1)
    own_queries = absorb(query_nope, query_rope, key_weight)
    maxima, totals, partials = shard_partial(
        lax.all_gather(own_queries, "seq", axis=2, tiled=True),
        latent_cache,
        limits,
        offset,
        factor,
        latent_width,
    )
    partials, maxima, totals = (partials, maxima, totals)
    sources = (partials[None], maxima[None], totals[None])
    gathered = merge_tuple(
        (
            lax.all_to_all(
                sources[0].astype(jnp.float32), "seq", split_axis=3, concat_axis=0, tiled=True
            ).astype(jnp.bfloat16),
            lax.all_to_all(sources[1], "seq", split_axis=3, concat_axis=0, tiled=True),
            lax.all_to_all(sources[2], "seq", split_axis=3, concat_axis=0, tiled=True),
        )
    )
    highest, summed, blended = joined((gathered[0], gathered[1], gathered[2]), "grp", join_pairs)
    values = up_project(blended.astype(jnp.bfloat16), value_weight)
    head_terms = jnp.dot(values, output_weight, preferred_element_type=jnp.float32)
    reduced = lax.psum_scatter(head_terms, "seq", scatter_dimension=2, tiled=True)
    return reduced.astype(jnp.bfloat16)


def solution(mesh):
    in_specs = (
        P(None, None, "seq", None),
        P(None, None, "seq", None),
        P(None, ("seq", "grp"), None),
        P(),
        P("seq", None, None),
        P("seq", None, None),
        P("seq", "grp"),
    )
    out_specs = P(None, None, ("grp", "seq"))
    return jax.shard_map(shards, mesh=mesh, in_specs=in_specs, out_specs=out_specs, check_vma=False)
```

profile of v0, /device:TPU:0, one launch (start us, length us, event | category | flops | bytes accessed | tf_op | source)
XLA Modules:
  0.0 212.3 jit_solution(17703678175560071938)
XLA Ops:
  6.5 0.9 copy.29
  7.5 0.7 copy-done
  8.1 1.1 fusion.18
  9.3 0.8 pad_maximum_fusion
  10.2 44.5 %all-gather.5.cloned.1.call-done = bf16[4,2,128,576]{3,0,1,2:T(4,128)(2,1)} async-done(((bf16[4,2,16,576]{3,0,1,2:T(4,128)(2,1)}), bf16[4,2,128,576]{3,0,1,2:T(4,128)(2,1)}) %all-gather.5.cloned.1.call-update) | async-done | bytes 1179664 | tf_op jit(solution)/shard_map/all_gather | solution.py:87
  54.7 2.4 %fusion.42 = (f32[4,2,128]{2,1,0:T(2,128)S(1)}, f32[4,2,128,256]{3,2,1,0:T(8,128)S(1)}) fusion(bf16[4,256,576]{1,2,0:T(8,128)(2,1)} %param.11, bf16[4,2,128,576]{3,0,1,2:T(4,128)(2,1)} %all-gather.5.cloned.1.call-done, pred[4,2,256]{2,1,0:T(4,128)(4,1)S(1)} %broadcast_compare_fusion), kind=kOutput, calls=%fused_computation.50 | convolution fusion | flops 302775296 | bytes 3414016 | tf_op jit(solution)/shard_map/bqhd,bpd->bqhp/dot_general | solution.py:22
  57.1 0.4 fusion.30
  57.5 0.2 copy.34
  57.7 0.8 reshape.85
  58.5 3.4 %all-to-all-start.1 = ((f32[8,1,128]{2,1,0:T(1,128)}), f32[8,1,128]{2,1,0:T(1,128)S(1)}, u32[]{:S(2)}, u32[]{:S(2)}) async-start(f32[8,1,128]{2,1,0:T(1,128)} %reshape.85), calls=%async_computation.1 | async-start | bytes 8192 | tf_op jit(solution)/shard_map/all_to_all | solution.py:102
  61.9 0.2 copy.31
  62.1 0.8 reshape.83
  62.9 5.5 %all-to-all-done.1 = f32[8,1,128]{2,1,0:T(1,128)S(1)} async-done(((f32[8,1,128]{2,1,0:T(1,128)}), f32[8,1,128]{2,1,0:T(1,128)S(1)}, u32[]{:S(2)}, u32[]{:S(2)}) %all-to-all-start.1) | async-done | bytes 4128 | tf_op jit(solution)/shard_map/all_to_all | solution.py:102
  68.4 3.3 %all-to-all-start = ((f32[8,1,128]{2,1,0:T(1,128)}), f32[8,1,128]{2,1,0:T(1,128)S(1)}, u32[]{:S(2)}, u32[]{:S(2)}) async-start(f32[8,1,128]{2,1,0:T(1,128)} %reshape.83), calls=%async_computation | async-start | bytes 8192 | tf_op jit(solution)/shard_map/all_to_all | solution.py:101
  71.7 1.7 fusion.11
  73.5 2.1 copy.38
  75.6 2.5 %all-to-all-done = f32[8,1,128]{2,1,0:T(1,128)S(1)} async-done(((f32[8,1,128]{2,1,0:T(1,128)}), f32[8,1,128]{2,1,0:T(1,128)S(1)}, u32[]{:S(2)}, u32[]{:S(2)}) %all-to-all-start) | async-done | bytes 4128 | tf_op jit(solution)/shard_map/all_to_all | solution.py:101
  78.1 3.6 %all-to-all-start.2 = ((bf16[1,4,2,128,512]{4,2,1,0,3:T(2,128)(2,1)}), bf16[1,4,2,128,512]{4,2,1,0,3:T(2,128)(2,1)S(1)}, u32[]{:S(2)}, u32[]{:S(2)}) async-start(bf16[1,4,2,128,512]{4,2,1,0,3:T(2,128)(2,1)} %copy.38), calls=%async_computation.2 | async-start | bytes 2097152 | tf_op jit(solution)/shard_map/all_to_all | solution.py:98
  81.7 0.5 broadcast.51
  82.2 0.7 reduce.2
  82.9 0.2 reshape.86
  83.1 1.6 copy.35
  84.7 0.7 reduce.1
  85.4 0.2 reshape.84
  85.6 0.9 copy.32
  86.6 1.8 fusion.40
  88.4 16.5 %all-to-all-done.2 = bf16[1,4,2,128,512]{4,2,1,0,3:T(2,128)(2,1)S(1)} async-done(((bf16[1,4,2,128,512]{4,2,1,0,3:T(2,128)(2,1)}), bf16[1,4,2,128,512]{4,2,1,0,3:T(2,128)(2,1)S(1)}, u32[]{:S(2)}, u32[]{:S(2)}) %all-to-all-start.2) | async-done | bytes 1048608 | tf_op jit(solution)/shard_map/all_to_all | solution.py:98
  104.9 2.3 %fusion.7 = f32[4,2,16,512]{3,1,0,2:T(2,128)S(1)} fusion(bf16[1,4,2,8,16,512]{5,2,1,4,3,0:T(2,128)(2,1)S(1)} %bitcast.108, f32[8,4,2,16]{2,1,3,0:T(4,128)} %get-tuple-element.201), kind=kLoop, calls=%fused_computation.13 | loop fusion | flops 1507328 | bytes 1314816 | tf_op jit(solution)/shard_map/reduce_sum | solution.py:45
  107.2 0.2 bitcast_divide_fusion
  107.3 0.9 copy.39
  108.3 0.1 copy.33
  108.4 0.1 copy.36
  108.5 5.2 %all-gather.1 = f32[16,2,16]{2,1,0:T(2,128)S(1)} all-gather(f32[4,2,16]{2,1,0:T(2,128)S(1)} %copy.36), channel_id=3, replica_groups=mesh['seq'=8,'grp'=4] {'grp'}, dimensions={0}, use_global_device_ids=true | all-gather | bytes 2560 | tf_op jit(solution)/shard_map/all_gather | solution.py:10
  113.7 5.2 %all-gather = f32[16,2,16]{2,1,0:T(2,128)S(1)} all-gather(f32[4,2,16]{2,1,0:T(2,128)S(1)} %copy.33), channel_id=2, replica_groups=mesh['seq'=8,'grp'=4] {'grp'}, dimensions={0}, use_global_device_ids=true | all-gather | bytes 2560 | tf_op jit(solution)/shard_map/all_gather | solution.py:10
  118.9 5.1 %all-gather.7.cloned.1.call-done = f32[4,4,2,16,512]{4,3,2,1,0:T(8,128)} async-done(((f32[1,4,2,16,512]{4,3,2,1,0:T(8,128)}), f32[4,4,2,16,512]{4,3,2,1,0:T(8,128)}) %all-gather.7.cloned.1.call-update) | async-done | bytes 1048592 | tf_op jit(solution)/shard_map/all_gather | solution.py:10
  124.0 1.0 slice_bitcast_fusion
  124.9 3.5 %while.19 = (s32[]{:T(128)}, f32[4,2,16]{2,1,0:T(2,128)S(1)}, f32[4,2,16]{2,1,0:T(2,128)S(1)}, f32[4,2,16,512]{3,2,1,0:T(8,128)S(1)}, f32[4,4,2,16]{3,2,1,0:T(2,...) while((s32[]{:T(128)}, f32[4,2,16]{2,1,0:T(2,128)S(1)}, ...), condition=%wide.region_6.7_spmd, body=%wide.region_5.6_spmd.sunk | while | flops 262917 | bytes 792207 | solution.py:15
  125.0 1.1 fusion.46
  126.2 1.1 fusion.46
  127.3 1.1 fusion.46
  128.4 2.0 fusion.24
  130.5 4.2 %fusion.3 = f32[4,2,1792]{2,0,1:T(4,128)S(1)} fusion(bf16[2048,1792]{1,0:T(8,128)(2,1)} %param.15, bf16[16,2,1,4,128]{4,3,2,1,0:T(4,128)(2,1)S(1)} %fusion.24), kind=kOutput, calls=%fused_computation.8 | convolution fusion | flops 58720256 | bytes 7430144 | tf_op jit(solution)/shard_map/dot_general | solution.py:107
  134.7 2.3 %copy.49 = f32[4,2,1792]{0,1,2:T(2,128)} copy(f32[4,2,1792]{2,0,1:T(4,128)S(1)} %fusion.3) | data formatting | bytes 114688
  137.0 3.1 %reshape.81 = f32[1792,8]{1,0:T(8,128)} reshape(f32[1792,2,4]{2,1,0:T(2,128)} %bitcast.107) | data formatting | bytes 114688
  140.1 63.9 %reduce-scatter.4.cloned.1.call-done = f32[224,8]{1,0:T(8,128)} async-done(((f32[1792,8]{1,0:T(8,128)}), f32[224,8]{1,0:T(8,128)}) %reduce-scatter.4.cloned.1.call-update) | async-done | bytes 7184
  204.0 1.0 reshape.82
  205.0 0.1 copy.50
  205.1 0.6 copy.43
  (20 shorter events, 0.5 us)
Async XLA Ops:
  6.5 1.6 copy-start
  6.5 3.5 %copy-start.1 = (s32[4]{0:T(128)S(1)}, s32[4]{0:T(128)}, u32[]{:S(2)}) copy-start(s32[4]{0:T(128)} %param.12) | copy-start | bytes 52
  6.5 48.2 %all-gather.5.cloned.1.call-start = ((), (), s32[]{:S(2)}) async-start(), calls=%async_computation.4 | async-start | bytes 1474560 | tf_op jit(solution)/shard_map/all_gather | solution.py:87
  58.5 9.9 %all-to-all-start.1 = ((f32[8,1,128]{2,1,0:T(1,128)}), f32[8,1,128]{2,1,0:T(1,128)S(1)}, u32[]{:S(2)}, u32[]{:S(2)}) async-start(f32[8,1,128]{2,1,0:T(1,128)} %reshape.85), calls=%async_computation.1 | async-start | bytes 8192 | tf_op jit(solution)/shard_map/all_to_all | solution.py:102
  68.4 9.7 %all-to-all-start = ((f32[8,1,128]{2,1,0:T(1,128)}), f32[8,1,128]{2,1,0:T(1,128)S(1)}, u32[]{:S(2)}, u32[]{:S(2)}) async-start(f32[8,1,128]{2,1,0:T(1,128)} %reshape.83), calls=%async_computation | async-start | bytes 8192 | tf_op jit(solution)/shard_map/all_to_all | solution.py:101
  78.1 26.8 %all-to-all-start.2 = ((bf16[1,4,2,128,512]{4,2,1,0,3:T(2,128)(2,1)}), bf16[1,4,2,128,512]{4,2,1,0,3:T(2,128)(2,1)S(1)}, u32[]{:S(2)}, u32[]{:S(2)}) async-start(bf16[1,4,2,128,512]{4,2,1,0,3:T(2,128)(2,1)} %copy.38), calls=%async_computation.2 | async-start | bytes 2097152 | tf_op jit(solution)/shard_map/all_to_all | solution.py:98
  81.6 42.3 %all-gather.7.cloned.1.call-start = ((), (), s32[]{:S(2)}) async-start(), calls=%async_computation.5 | async-start | bytes 1310720 | tf_op jit(solution)/shard_map/all_gather | solution.py:10
  108.2 95.8 %reduce-scatter.4.cloned.1.call-start = ((), (), s32[]{:S(2)}) async-start(), calls=%async_computation.6 | async-start | bytes 1032192
Sparse Core Ops, SparseCore 0:
  10.2 44.5 all-gather.4
  108.4 15.5 all-gather.6
  140.3 63.6 reduce-scatter.3
where the time goes:
time: 213 us; the launch traced here: 212 us
  waiting for transfers between devices  138 us (65%)
  local copies, waits for them, and re-layouts  18.2 us (9%)
  between operations  13.3 us (6%)
  matrix products  11.5 us (5%)
  starting transfers between devices  10.4 us (5%)
  blocking collectives  10.4 us (5%)
  other arithmetic  10.3 us (5%)
    unnamed x4, waiting for transfers between devices  63.9 us
    all_gather x1, waiting for transfers between devices, shards(): lax.all_gather(own_queries, 'seq', axis=2, tiled=True)  44.5 us
    all_to_all x1, waiting for transfers between devices, shards(): lax.all_to_all(sources[0].astype(jnp.float32), 'seq', split_axis=3, conca...  16.5 us
    all_gather x2, blocking collectives, joined(): gathered = jax.tree.map(lambda a: lax.all_gather(a, axis), part)  10.4 us
    unnamed x13, local copies, waits for them, and re-layouts  10.2 us
    all_to_all x1, waiting for transfers between devices, shards(): lax.all_to_all(sources[2], 'seq', split_axis=3, concat_axis=0, tiled=True)  5.53 us
    all_gather x1, waiting for transfers between devices, joined(): gathered = jax.tree.map(lambda a: lax.all_gather(a, axis), part)  5.1 us
  transfers between devices with their start and end apart: 6, of which 6 were waited for; matrix products, arithmetic and copies ran while one was open for 6% of the time, Pallas kernels for 0%

commit v1 on v0

--- a/solution.py
+++ b/solution.py
@@ -4,6 +4,30 @@
 from jax.sharding import PartitionSpec as P
 
 NEGATIVE = -1e30
+
+
+def in_blocks(x, dim, length):
+    lengths = x.shape
+    blocks = x.reshape(*lengths[:dim], length, lengths[dim] // length, *lengths[dim + 1 :])
+    return jnp.moveaxis(blocks, dim, 0)
+
+
+def laid_out(blocks, dim):
+    shape = list(blocks.shape[1:])
+    shape[dim] *= blocks.shape[0]
+    return jnp.moveaxis(blocks, 0, dim).reshape(shape)
+
+
+def exchange_directly(array, axis, split_dim, concat_dim):
+    length, index = (lax.axis_size(axis), lax.axis_index(axis))
+    parts = in_blocks(array, split_dim, length)
+    out = parts
+    for hop in range(1, length):
+        target, source = ((index + hop) % length, (index - hop) % length)
+        sent = lax.dynamic_index_in_dim(parts, target, 0)
+        theirs = lax.ppermute(sent, axis, [(i, (i + hop) % length) for i in range(length)])
+        out = lax.dynamic_update_slice_in_dim(out, theirs, source, axis=0)
+    return laid_out(out, concat_dim)
 
 
 def joined(part, axis, combine):
@@ -95,9 +119,7 @@
     sources = (partials[None], maxima[None], totals[None])
     gathered = merge_tuple(
         (
-            lax.all_to_all(
-                sources[0].astype(jnp.float32), "seq", split_axis=3, concat_axis=0, tiled=True
-            ).astype(jnp.bfloat16),
+            exchange_directly(sources[0].astype(jnp.float32), "seq", 3, 0).astype(jnp.bfloat16),
             lax.all_to_all(sources[1], "seq", split_axis=3, concat_axis=0, tiled=True),
             lax.all_to_all(sources[2], "seq", split_axis=3, concat_axis=0, tiled=True),
         )

time: 213 us -> 207 us (0.972)
  waiting for transfers between devices: 138 us -> 119 us
  starting transfers between devices: 10.4 us -> 19.4 us
  local copies, waits for them, and re-layouts: 18.2 us -> 22.9 us
    all_to_all x1 -> x0, waiting for transfers between devices: 16.5 us -> none  [shards(): lax.all_to_all(sources[0].astype(jnp.float32), 'seq', split_axis=3, conca...]
    ppermute x0 -> x7, starting transfers between devices: none -> 12.6 us  [exchange_directly(): lax.ppermute(sent, axis, [(i, (i + hop) % length) for i in range(length)])]
    dynamic_update_slice x0 -> x7, local copies, waits for them, and re-layouts: none -> 4.62 us  [exchange_directly(): out = lax.dynamic_update_slice_in_dim(out, theirs, source, axis=0)]
    all_to_all x1 -> x0, starting transfers between devices: 3.56 us -> none  [shards(): lax.all_to_all(sources[0].astype(jnp.float32), 'seq', split_axis=3, conca...]
    all_to_all x1, waiting for transfers between devices: 2.53 us -> 0.01 us  [shards(): lax.all_to_all(sources[1], 'seq', split_axis=3, concat_axis=0, tiled=True)]
    unnamed x13 -> x15, local copies, waits for them, and re-layouts: 10.2 us -> 11.2 us
  transfers between devices with their start and end apart: 6 -> 12, of which waited for: 6 -> 4; matrix products, arithmetic and copies ran while one was open for 6% -> 8% of each run, Pallas kernels for 0% -> 0%
where the time goes in v1:
time: 207 us; the launch traced here: 206 us
  waiting for transfers between devices  119 us (57%)
  local copies, waits for them, and re-layouts  22.9 us (11%)
  starting transfers between devices  19.4 us (9%)
  between operations  13.6 us (7%)
  matrix products  11.8 us (6%)
  blocking collectives  10.4 us (5%)
  other arithmetic  8.73 us (4%)
    unnamed x4, waiting for transfers between devices  63.9 us
    all_gather x1, waiting for transfers between devices, shards(): lax.all_gather(own_queries, 'seq', axis=2, tiled=True)  44.3 us
    ppermute x7, starting transfers between devices, exchange_directly(): lax.ppermute(sent, axis, [(i, (i + hop) % length) for i in range(length)])  12.6 us
    unnamed x15, local copies, waits for them, and re-layouts  11.2 us
    all_gather x2, blocking collectives, joined(): gathered = jax.tree.map(lambda a: lax.all_gather(a, axis), part)  10.4 us
    all_gather x1, waiting for transfers between devices, joined(): gathered = jax.tree.map(lambda a: lax.all_gather(a, axis), part)  7.17 us
    dynamic_update_slice x7, local copies, waits for them, and re-layouts, exchange_directly(): out = lax.dynamic_update_slice_in_dim(out, theirs, source, axis=0)  4.62 us
    dot_general x1, matrix products, shards(): jnp.dot(values, output_weight, preferred_element_type=jnp.float32)  4.22 us
  transfers between devices with their start and end apart: 12, of which 4 were waited for; matrix products, arithmetic and copies ran while one was open for 8% of the time, Pallas kernels for 0%

profile of v1, /device:TPU:0, one launch (start us, length us, event | category | flops | bytes accessed | tf_op | source)
XLA Modules:
  0.0 205.8 jit_solution(10166744433918149020)
XLA Ops:
  6.5 0.9 copy.29
  7.5 0.7 copy-done
  8.1 1.1 fusion.15
  9.3 0.8 pad_maximum_fusion
  10.5 44.3 %all-gather.5.cloned.1.call-done = bf16[4,2,128,576]{3,0,1,2:T(4,128)(2,1)} async-done(((bf16[4,2,16,576]{3,0,1,2:T(4,128)(2,1)}), bf16[4,2,128,576]{3,0,1,2:T(4,128)(2,1)}) %all-gather.5.cloned.1.call-update) | async-done | bytes 1179664 | tf_op jit(solution)/shard_map/all_gather | solution.py:111
  54.8 2.4 %fusion.39 = (f32[4,2,128]{2,1,0:T(2,128)S(1)}, f32[4,2,128,256]{3,2,1,0:T(8,128)S(1)}) fusion(bf16[4,256,576]{1,2,0:T(8,128)(2,1)} %param.11, bf16[4,2,128,576]{3,0,1,2:T(4,128)(2,1)} %all-gather.5.cloned.1.call-done, pred[4,2,256]{2,1,0:T(4,128)(4,1)S(1)} %broadcast_compare_fusion), kind=kOutput, calls=%fused_computation.62 | convolution fusion | flops 302775296 | bytes 3414016 | tf_op jit(solution)/shard_map/bqhd,bpd->bqhp/dot_general | solution.py:46
  57.1 1.0 copy-done.1
  58.7 0.8 reshape.132
  59.5 3.4 %all-to-all-start.1 = ((f32[8,1,128]{2,1,0:T(1,128)}), f32[8,1,128]{2,1,0:T(1,128)S(1)}, u32[]{:S(2)}, u32[]{:S(2)}) async-start(f32[8,1,128]{2,1,0:T(1,128)} %reshape.132), calls=%async_computation.1 | async-start | bytes 8192 | tf_op jit(solution)/shard_map/all_to_all | solution.py:124
  62.9 2.0 divide_convert_fusion
  65.1 0.8 reshape.130
  65.9 3.5 %all-to-all-done.1 = f32[8,1,128]{2,1,0:T(1,128)S(1)} async-done(((f32[8,1,128]{2,1,0:T(1,128)}), f32[8,1,128]{2,1,0:T(1,128)S(1)}, u32[]{:S(2)}, u32[]{:S(2)}) %all-to-all-start.1) | async-done | bytes 4128 | tf_op jit(solution)/shard_map/all_to_all | solution.py:124
  69.4 3.3 %all-to-all-start = ((f32[8,1,128]{2,1,0:T(1,128)}), f32[8,1,128]{2,1,0:T(1,128)S(1)}, u32[]{:S(2)}, u32[]{:S(2)}) async-start(f32[8,1,128]{2,1,0:T(1,128)} %reshape.130), calls=%async_computation | async-start | bytes 8192 | tf_op jit(solution)/shard_map/all_to_all | solution.py:123
  72.8 1.0 dynamic-slice_bitcast_fusion
  73.7 1.9 collective-permute-start
  75.6 1.5 collective-permute-start.1
  77.1 2.4 %collective-permute-start.2 = (bf16[1,1,4,2,16,512]{5,4,3,2,1,0:T(8,128)(2,1)}, bf16[1,1,4,2,16,512]{5,4,3,2,1,0:T(8,128)(2,1)}, u32[]{:S(2)}, u32[]{:S(2)}) collective-permute-start(bf16[1,1,4,2,16,512]{5,4,3,2,1,0:T(8,128)(2,1)} %get-tuple-element.205), channel_id=1, source_target_pairs={{0,12},{4,16},{8,20},{12,24},{16,28},{20,0},{24,4},{28,8},{1,13},{... | collective-permute-start | bytes 393224 | tf_op jit(solution)/shard_map/ppermute | solution.py:28
  79.4 1.4 collective-permute-start.3
  80.9 2.4 %collective-permute-start.4 = (bf16[1,1,4,2,16,512]{5,4,3,2,1,0:T(8,128)(2,1)}, bf16[1,1,4,2,16,512]{5,4,3,2,1,0:T(8,128)(2,1)}, u32[]{:S(2)}, u32[]{:S(2)}) collective-permute-start(bf16[1,1,4,2,16,512]{5,4,3,2,1,0:T(8,128)(2,1)} %get-tuple-element.203), channel_id=1, source_target_pairs={{0,20},{4,24},{8,28},{12,0},{16,4},{20,8},{24,12},{28,16},{1,21},{... | collective-permute-start | bytes 393224 | tf_op jit(solution)/shard_map/ppermute | solution.py:28
  83.7 0.6 reduce.2
  84.5 1.6 copy.35
  86.1 0.6 reduce.1
  86.9 0.9 copy.32
  87.9 1.8 fusion.37
  89.6 1.2 copy.37
  90.9 1.5 collective-permute-start.5
  92.4 0.9 bitcast_dynamic-update-slice_fusion.6
  93.4 1.5 collective-permute-start.6
  94.9 0.9 bitcast_dynamic-update-slice_fusion.5
  95.8 0.9 bitcast_dynamic-update-slice_fusion.4
  96.7 0.9 bitcast_dynamic-update-slice_fusion.3
  97.7 0.9 bitcast_dynamic-update-slice_fusion.2
  98.9 0.8 bitcast_divide_fusion
  99.9 5.2 %all-gather.1 = f32[16,2,16]{2,1,0:T(2,128)S(1)} all-gather(f32[4,2,16]{2,1,0:T(2,128)S(1)} %copy.36), channel_id=3, replica_groups=mesh['seq'=8,'grp'=4] {'grp'}, dimensions={0}, use_global_device_ids=true | all-gather | bytes 2560 | tf_op jit(solution)/shard_map/all_gather | solution.py:34
  105.1 5.2 %all-gather = f32[16,2,16]{2,1,0:T(2,128)S(1)} all-gather(f32[4,2,16]{2,1,0:T(2,128)S(1)} %copy.33), channel_id=2, replica_groups=mesh['seq'=8,'grp'=4] {'grp'}, dimensions={0}, use_global_device_ids=true | all-gather | bytes 2560 | tf_op jit(solution)/shard_map/all_gather | solution.py:34
  110.3 7.2 %all-gather.7.cloned.1.call-done = f32[4,4,2,16,512]{4,3,2,1,0:T(8,128)} async-done(((f32[1,4,2,16,512]{4,3,2,1,0:T(8,128)}), f32[4,4,2,16,512]{4,3,2,1,0:T(8,128)}) %all-gather.7.cloned.1.call-update) | async-done | bytes 1048592 | tf_op jit(solution)/shard_map/all_gather | solution.py:34
  117.5 1.0 slice_bitcast_fusion
  118.4 3.5 %while.19 = (s32[]{:T(128)}, f32[4,2,16]{2,1,0:T(2,128)S(1)}, f32[4,2,16]{2,1,0:T(2,128)S(1)}, f32[4,2,16,512]{3,2,1,0:T(8,128)S(1)}, f32[4,4,2,16]{3,2,1,0:T(2,...) while((s32[]{:T(128)}, f32[4,2,16]{2,1,0:T(2,128)S(1)}, ...), condition=%wide.region_6.7_spmd, body=%wide.region_5.6_spmd.sunk | while | flops 262917 | bytes 792215 | solution.py:39
  118.5 1.1 fusion.43
  119.6 1.1 fusion.43
  120.8 1.1 fusion.43
  121.9 2.0 fusion.21
  124.0 4.2 %fusion.3 = f32[4,2,1792]{2,0,1:T(4,128)S(1)} fusion(bf16[2048,1792]{1,0:T(8,128)(2,1)} %param.15, bf16[16,2,1,4,128]{4,3,2,1,0:T(4,128)(2,1)S(1)} %fusion.21), kind=kOutput, calls=%fused_computation.8 | convolution fusion | flops 58720256 | bytes 7430144 | tf_op jit(solution)/shard_map/dot_general | solution.py:129
  128.2 2.3 %copy.49 = f32[4,2,1792]{0,1,2:T(2,128)} copy(f32[4,2,1792]{2,0,1:T(4,128)S(1)} %fusion.3) | data formatting | bytes 114688
  130.5 3.1 %reshape.128 = f32[1792,8]{1,0:T(8,128)} reshape(f32[1792,2,4]{2,1,0:T(2,128)} %bitcast.129) | data formatting | bytes 114688
  133.6 63.9 %reduce-scatter.4.cloned.1.call-done = f32[224,8]{1,0:T(8,128)} async-done(((f32[1792,8]{1,0:T(8,128)}), f32[224,8]{1,0:T(8,128)}) %reduce-scatter.4.cloned.1.call-update) | async-done | bytes 7184
  197.5 1.0 reshape.129
  198.6 0.6 copy.43
  (41 shorter events, 2.7 us)
Async XLA Ops:
  6.5 1.6 copy-start
  6.5 3.8 %copy-start.2 = (s32[4]{0:T(128)S(1)}, s32[4]{0:T(128)}, u32[]{:S(2)}) copy-start(s32[4]{0:T(128)} %param.12) | copy-start | bytes 52
  6.5 48.2 %all-gather.5.cloned.1.call-start = ((), (), s32[]{:S(2)}) async-start(), calls=%async_computation.3 | async-start | bytes 1474560 | tf_op jit(solution)/shard_map/all_gather | solution.py:111
  57.1 1.0 copy-start.1
  59.5 9.9 %all-to-all-start.1 = ((f32[8,1,128]{2,1,0:T(1,128)}), f32[8,1,128]{2,1,0:T(1,128)S(1)}, u32[]{:S(2)}, u32[]{:S(2)}) async-start(f32[8,1,128]{2,1,0:T(1,128)} %reshape.132), calls=%async_computation.1 | async-start | bytes 8192 | tf_op jit(solution)/shard_map/all_to_all | solution.py:124
  69.4 16.7 %all-to-all-start = ((f32[8,1,128]{2,1,0:T(1,128)}), f32[8,1,128]{2,1,0:T(1,128)S(1)}, u32[]{:S(2)}, u32[]{:S(2)}) async-start(f32[8,1,128]{2,1,0:T(1,128)} %reshape.130), calls=%async_computation | async-start | bytes 8192 | tf_op jit(solution)/shard_map/all_to_all | solution.py:123
  72.7 44.7 %all-gather.7.cloned.1.call-start = ((), (), s32[]{:S(2)}) async-start(), calls=%async_computation.4 | async-start | bytes 1310720 | tf_op jit(solution)/shard_map/all_gather | solution.py:34
  73.7 17.2 %collective-permute-start = (bf16[1,1,4,2,16,512]{5,4,3,2,1,0:T(8,128)(2,1)}, bf16[1,1,4,2,16,512]{5,4,3,2,1,0:T(8,128)(2,1)}, u32[]{:S(2)}, u32[]{:S(2)}) collective-permute-start(bf16[1,1,4,2,16,512]{5,4,3,2,1,0:T(8,128)(2,1)} %get-tuple-element.207), channel_id=1, source_target_pairs={{0,4},{4,8},{8,12},{12,16},{16,20},{20,24},{24,28},{28,0},{1,5},{5... | collective-permute-start | bytes 393224 | tf_op jit(solution)/shard_map/ppermute | solution.py:28
  75.6 17.8 %collective-permute-start.1 = (bf16[1,1,4,2,16,512]{5,4,3,2,1,0:T(8,128)(2,1)}, bf16[1,1,4,2,16,512]{5,4,3,2,1,0:T(8,128)(2,1)}, u32[]{:S(2)}, u32[]{:S(2)}) collective-permute-start(bf16[1,1,4,2,16,512]{5,4,3,2,1,0:T(8,128)(2,1)} %get-tuple-element.206), channel_id=1, source_target_pairs={{0,8},{4,12},{8,16},{12,20},{16,24},{20,28},{24,0},{28,4},{1,9},{5... | collective-permute-start | bytes 393224 | tf_op jit(solution)/shard_map/ppermute | solution.py:28
  77.1 18.7 %collective-permute-start.2 = (bf16[1,1,4,2,16,512]{5,4,3,2,1,0:T(8,128)(2,1)}, bf16[1,1,4,2,16,512]{5,4,3,2,1,0:T(8,128)(2,1)}, u32[]{:S(2)}, u32[]{:S(2)}) collective-permute-start(bf16[1,1,4,2,16,512]{5,4,3,2,1,0:T(8,128)(2,1)} %get-tuple-element.205), channel_id=1, source_target_pairs={{0,12},{4,16},{8,20},{12,24},{16,28},{20,0},{24,4},{28,8},{1,13},{... | collective-permute-start | bytes 393224 | tf_op jit(solution)/shard_map/ppermute | solution.py:28
  79.4 17.3 %collective-permute-start.3 = (bf16[1,1,4,2,16,512]{5,4,3,2,1,0:T(8,128)(2,1)}, bf16[1,1,4,2,16,512]{5,4,3,2,1,0:T(8,128)(2,1)}, u32[]{:S(2)}, u32[]{:S(2)}) collective-permute-start(bf16[1,1,4,2,16,512]{5,4,3,2,1,0:T(8,128)(2,1)} %get-tuple-element.204), channel_id=1, source_target_pairs={{0,16},{4,20},{8,24},{12,28},{16,0},{20,4},{24,8},{28,12},{1,17},{... | collective-permute-start | bytes 393224 | tf_op jit(solution)/shard_map/ppermute | solution.py:28
  80.9 16.8 %collective-permute-start.4 = (bf16[1,1,4,2,16,512]{5,4,3,2,1,0:T(8,128)(2,1)}, bf16[1,1,4,2,16,512]{5,4,3,2,1,0:T(8,128)(2,1)}, u32[]{:S(2)}, u32[]{:S(2)}) collective-permute-start(bf16[1,1,4,2,16,512]{5,4,3,2,1,0:T(8,128)(2,1)} %get-tuple-element.203), channel_id=1, source_target_pairs={{0,20},{4,24},{8,28},{12,0},{16,4},{20,8},{24,12},{28,16},{1,21},{... | collective-permute-start | bytes 393224 | tf_op jit(solution)/shard_map/ppermute | solution.py:28
  90.9 7.7 %collective-permute-start.5 = (bf16[1,1,4,2,16,512]{5,4,3,2,1,0:T(8,128)(2,1)}, bf16[1,1,4,2,16,512]{5,4,3,2,1,0:T(8,128)(2,1)S(1)}, u32[]{:S(2)}, u32[]{:S(2)}) collective-permute-start(bf16[1,1,4,2,16,512]{5,4,3,2,1,0:T(8,128)(2,1)} %get-tuple-element.208), channel_id=1, source_target_pairs={{0,24},{4,28},{8,0},{12,4},{16,8},{20,12},{24,16},{28,20},{1,25},{... | collective-permute-start | bytes 393224 | tf_op jit(solution)/shard_map/ppermute | solution.py:28
  93.4 5.3 %collective-permute-start.6 = (bf16[1,1,4,2,16,512]{5,4,3,2,1,0:T(8,128)(2,1)}, bf16[1,1,4,2,16,512]{5,4,3,2,1,0:T(8,128)(2,1)S(1)}, u32[]{:S(2)}, u32[]{:S(2)}) collective-permute-start(bf16[1,1,4,2,16,512]{5,4,3,2,1,0:T(8,128)(2,1)} %get-tuple-element.202), channel_id=1, source_target_pairs={{0,28},{4,0},{8,4},{12,8},{16,12},{20,16},{24,20},{28,24},{1,29},{... | collective-permute-start | bytes 393224 | tf_op jit(solution)/shard_map/ppermute | solution.py:28
  99.7 97.8 %reduce-scatter.4.cloned.1.call-start = ((), (), s32[]{:S(2)}) async-start(), calls=%async_computation.5 | async-start | bytes 1032192
Sparse Core Ops, SparseCore 0:
  10.2 44.5 all-gather.4
  99.9 17.5 all-gather.6
  133.7 63.7 reduce-scatter.3
